TPU v7x, 16 devices: a whole 2x2x2 slice. The times are simulated.
16 devices in a mesh: data: 16 (over z, y, x, core).
Axes of the slice: x: 2, y: 2, z: 2, core: 2. Of those that a mesh axis runs over, the one named last changes fastest.
Arguments:
- act_in: bfloat16 [65536, 896], P('data')
- grad_out: bfloat16 [65536, 896], P('data')
- w_up1: bfloat16 [896, 4864], replicated
- w_down1: bfloat16 [4864, 896], replicated
- w_up2: bfloat16 [896, 4864], replicated
- w_down2: bfloat16 [4864, 896], replicated
- master_up1: float32 [896, 4864], P('data')
- master_down1: float32 [4864, 896], P('data')
- master_up2: float32 [896, 4864], P('data')
- master_down2: float32 [4864, 896], P('data')
- mom_up1: float32 [896, 4864], P('data')
- mom_down1: float32 [4864, 896], P('data')
- mom_up2: float32 [896, 4864], P('data')
- mom_down2: float32 [4864, 896], P('data')
- vel_up1: float32 [896, 4864], P('data')
- vel_down1: float32 [4864, 896], P('data')
- vel_up2: float32 [896, 4864], P('data')
- vel_down2: float32 [4864, 896], P('data')
- learn_rate: float32 [], replicated
- clip_norm: float32 [], replicated
Outputs:
- output 1: bfloat16 [896, 4864], replicated
- output 2: bfloat16 [4864, 896], replicated
- output 3: bfloat16 [896, 4864], replicated
- output 4: bfloat16 [4864, 896], replicated
- output 5: float32 [896, 4864], P('data')
- output 6: float32 [4864, 896], P('data')
- output 7: float32 [896, 4864], P('data')
- output 8: float32 [4864, 896], P('data')
- output 9: float32 [896, 4864], P('data')
- output 10: float32 [4864, 896], P('data')
- output 11: float32 [896, 4864], P('data')
- output 12: float32 [4864, 896], P('data')
- output 13: float32 [896, 4864], P('data')
- output 14: float32 [4864, 896], P('data')
- output 15: float32 [896, 4864], P('data')
- output 16: float32 [4864, 896], P('data')
- output 17: float32 [], replicated
All inputs are finite; a program needn't handle non-finite values.
Results may differ from a plain program's by a relative error of at most 0.010218.
Values are sent between devices in bfloat16 or wider.
A program may use at most 1 GiB of HBM per device.

v0:
```python
import functools
import math
import jax
import jax.numpy as jnp
from jax import lax
from jax.experimental import pallas as pl
from jax.experimental.pallas import tpu as pltpu
from jax.sharding import PartitionSpec as P

ROOT_HALF = math.sqrt(0.5)
INV_ROOT_TAU = 1.0 / math.sqrt(2.0 * math.pi)
F32, BF16 = jnp.float32, jnp.bfloat16
HBM = pl.BlockSpec(memory_space=pltpu.HBM)
VMEM_MAX = 64 * 1024 * 1024 - 65536
BLOCKS = 8
TURNS = 8
RING = 6


def dot_nn(a, b):
    return lax.dot_general(a, b, (((1,), (0,)), ((), ())), preferred_element_type=F32)


def dot_nt(a, b):
    return lax.dot_general(a, b, (((1,), (1,)), ((), ())), preferred_element_type=F32)


def gelu(z):
    return z * (0.5 * (1.0 + lax.erf(z * ROOT_HALF)))


def at_most(j, bound):
    return jnp.minimum(j, bound)


def aligned(j, size):
    return pl.ds(pl.multiple_of(j * size, size), size)


def kernel_a(cfg, x_hbm, e_hbm, w1_hbm, w3_hbm, w2_hbm, z_hbm, ut_hbm, xt_hbm, et_hbm, w3t_hbm,
             xt, uacc, zout, w1t_v, w1_in, x_in, w1, w2, w2t, w3_in, w3_out, e_in, e_out, h0, h1,
             wsem, xsem, esem, vsem, zsem, osem):
    nt, nr, rb, tr, tb, ft, d, nd = cfg
    hb = (h0, h1)
    width = ft // nd

    def w1copy(q):
        slot = lax.rem(q, RING)
        return pltpu.make_async_copy(w1_hbm.at[:, aligned(q, ft)], w1_in.at[slot], wsem.at[slot])

    def xcopy(r):
        slot = lax.rem(r, RING)
        return pltpu.make_async_copy(x_hbm.at[aligned(r, tb), :], x_in.at[slot], xsem.at[slot])

    def w2copy(j):
        slot = lax.rem(j, 2)
        return pltpu.make_async_copy(w2_hbm.at[:, j], w2.at[slot], vsem.at[0, slot])

    def w3copy(j):
        slot = lax.rem(j, 2)
        return pltpu.make_async_copy(w3_hbm.at[:, aligned(j, ft)], w3_in.at[slot], vsem.at[1, slot])

    def w3store(j):
        slot = lax.rem(j, 2)
        return pltpu.make_async_copy(w3_out.at[slot], w3t_hbm.at[aligned(j, ft), :], osem.at[0, slot])

    def ecopy(r):
        slot = lax.rem(r, 2)
        return pltpu.make_async_copy(e_hbm.at[aligned(r, tb), :], e_in.at[slot], esem.at[slot])

    def estore(r):
        slot = lax.rem(r, 2)
        return pltpu.make_async_copy(e_out.at[slot], et_hbm.at[:, aligned(r, tb)], osem.at[1, slot])

    def zstore(j):
        slot = lax.rem(j, 2)
        return pltpu.make_async_copy(zout.at[slot], z_hbm.at[j], zsem.at[slot])

    for q in range(min(RING, nt)):
        w1copy(q).start()
    for r in range(min(RING, tr)):
        xcopy(r).start()
    for c in (w2copy(0), w3copy(0), ecopy(0)):
        c.start()

    def zero(r, _):
        uacc[:, aligned(r, rb)] = jnp.zeros((d, rb), F32)
        return 0
    lax.fori_loop(0, nr, zero, 0)

    def turn_w1(q, _):
        w1copy(q).wait()
        w1t_v[aligned(q, ft), :] = w1_in[lax.rem(q, RING)].T
        @pl.when(q + RING < nt)
        def _():
            w1copy(q + RING).start()
        return 0
    lax.fori_loop(0, nt, turn_w1, 0)

    def turn_x(r, _):
        xcopy(r).wait()
        xt[:, aligned(r, tb)] = x_in[lax.rem(r, RING)].T
        @pl.when(r + RING < tr)
        def _():
            xcopy(r + RING).start()
        return 0
    lax.fori_loop(0, tr, turn_x, 0)
    xt_store = pltpu.make_async_copy(xt, xt_hbm, osem.at[2, 0])
    xt_store.start()

    def pick_w1(j, slot):
        for k in range(nd):
            w1[slot, k * width:(k + 1) * width, :] = w1t_v[aligned(k * nt + j, width), :]
    pick_w1(0, 0)

    def tile(j, _):
        slot = lax.rem(j, 2)
        nslot = 1 - slot
        @pl.when(j >= 2)
        def _():
            zstore(j - 2).wait()
            w3store(j - 2).wait()
        @pl.when(jnp.logical_and(j >= 2, j < tr + 2))
        def _():
            estore(j - 2).wait()
        w2copy(j).wait()
        w3copy(j).wait()
        @pl.when(j < tr)
        def _():
            ecopy(j).wait()
        @pl.when(j + 1 < nt)
        def _():
            w2copy(j + 1).start()
            w3copy(j + 1).start()
        @pl.when(j + 1 < min(tr, nt))
        def _():
            ecopy(j + 1).start()

        def cols(r):
            return pl.ds(r * rb, rb)
        def front(r):
            zout[slot, :, cols(r)] = dot_nn(w1[slot], xt[:, cols(r)])
        def middle(r):
            hb[r % 2][...] = gelu(zout[slot, :, cols(r)]).astype(BF16)
        def back(r):
            uacc[:, cols(r)] += dot_nn(w2t[...], hb[r % 2][...])
        front(0)
        w2t[...] = w2[slot].reshape(ft, d).T
        for r in range(nr):
            middle(r)
            if r + 1 < nr:
                front(r + 1)
            if r >= 1:
                back(r - 1)
            if r == 0:
                pick_w1(at_most(j + 1, nt - 1), nslot)
            if r == 1:
                w3_out[slot] = w3_in[slot].T
            if r == nr - 2:
                e_out[slot] = e_in[slot].T
        back(nr - 1)
        zstore(j).start()
        w3store(j).start()
        @pl.when(j < tr)
        def _():
            estore(j).start()
        return 0
    lax.fori_loop(0, nt, tile, 0)
    xt_store.wait()

    def finish(r, _):
        xt[:, aligned(r, rb)] = uacc[:, aligned(r, rb)].astype(BF16)
        return 0
    lax.fori_loop(0, nr, finish, 0)
    ut_store = pltpu.make_async_copy(xt, ut_hbm, osem.at[2, 1])
    ut_store.start()
    for j in (nt - 2, nt - 1):
        zstore(j).wait()
        w3store(j).wait()
        if j < tr:
            estore(j).wait()
    for r in range(nt, tr):
        ecopy(r).start()
        ecopy(r).wait()
        e_out[r % 2] = e_in[r % 2].T
        estore(r).start()
        estore(r).wait()
    ut_store.wait()


def forward_one(x, e, w1, w3, w2r):
    t, d = x.shape
    nd, nt, rows2, _ = w2r.shape
    ft, nr, tr = nd * rows2, BLOCKS, TURNS
    rb, tb = t // nr, t // tr
    V, D = pltpu.VMEM, pltpu.SemaphoreType.DMA
    S = jax.ShapeDtypeStruct
    return pl.pallas_call(
        functools.partial(kernel_a, (nt, nr, rb, tr, tb, ft, d, nd)),
        out_shape=(S((nt, ft, t), F32), S((d, t), BF16), S((d, t), BF16), S((d, t), BF16), S((nt * ft, d), BF16)),
        in_specs=[HBM] * 5, out_specs=(HBM,) * 5,
        scratch_shapes=[
            V((d, t), BF16), V((d, t), F32), V((2, ft, t), F32), V((nt * ft, d), BF16), V((RING, d, ft), BF16), V((RING, tb, d), BF16),
            V((2, ft, d), BF16), V((2, nd, rows2, d), BF16), V((d, ft), BF16), V((2, d, ft), BF16), V((2, ft, d), BF16),
            V((2, tb, d), BF16), V((2, d, tb), BF16), V((ft, rb), BF16), V((ft, rb), BF16),
            D((RING,)), D((RING,)), D((2,)), D((2, 2)), D((2,)), D((3, 2))],
        compiler_params=pltpu.CompilerParams(vmem_limit_bytes=VMEM_MAX),
        name="forward_one",
    )(x, e, w1, w3, w2r)


MESH = pl.DeviceIdType.MESH

def gelu_pair(pre):
    normal_cdf = 0.5 * (1.0 + lax.erf(pre * ROOT_HALF))
    density = jnp.exp(-0.5 * pre * pre) * INV_ROOT_TAU
    return pre * normal_cdf, normal_cdf + pre * density

def flip(value, step):
    return value + step * (1 - 2 * lax.rem(lax.div(value, step), 2))

def position():
    me = lax.axis_index("data")
    chip = lax.div(me, 2)
    steps = [(1 << k) * (1 - 2 * lax.rem(lax.div(chip, 1 << k), 2)) for k in range(AXES)]
    return me, lax.rem(me, 2), chip, steps


def hop(steps, kind, place, j):
    axis = lax.rem(j + ORDERS[kind][place], AXES)
    return steps[0] * lax.div((2 - axis) * (1 - axis), 2) + steps[1] * axis * (2 - axis) + steps[2] * lax.div(axis * (axis - 1), 2)


def relative(hops, p):
    return sum((hops[place] for place in range(AXES) if (p >> (AXES - 1 - place)) & 1), 0)


AXES = 3


def meet(peers):
    barrier = pltpu.get_barrier_semaphore()
    for peer in peers:
        pl.semaphore_signal(barrier, inc=1, device_id=(peer,), device_id_type=MESH)
    pl.semaphore_wait(barrier, len(peers))


ORDERS = ((0, 2, 1), (1, 2, 0))
PARTS = 8
BACK_BLOCKS = 4
BEGUN = 2
TURN = 128
SEEN = (3, 6, 9, 12)
DEPTH = (2, 6, 6, 6)
LAST = len(SEEN) - 1
HOLD = 3

def kernel_bc(cfg, ut_hbm, et_hbm, xt_hbm, z_hbm, w3_hbm, w4_hbm, w2_hbm,
              gu_hbm, gd_hbm, nrm_ref,
              act, side, euacc, wa, wb, wat, zb0, zb1, eb0, eb1, hb0, hb1, qb0, qb1,
              gu, gt, gd, r0u, r0d, a0u, a0d, a1u, a1d, a2u, a2d, r1u, r1d, r2u, r2d, r3u, r3d, fu, fd, nu, nd_acc,
              insem, wsem, zsem, ssem, rsem, fsem):
    nt, nr, nc, t, ft, d, nd = cfg
    rb, rc = t // nr, t // nc
    total = 2 * nt
    me, core, chip, steps = position()
    partner = flip(me, 1)
    zb, eb, hb, qb = (zb0, zb1), (eb0, eb1), (hb0, hb1), (qb0, qb1)
    G, R, ACC, FIN, NRM, OUT = (gu, gd), ((r0u, r1u, r2u, r3u), (r0d, r1d, r2d, r3d)), ((a0u, a1u, a2u), (a0d, a1d, a2d)), (fu, fd), (nu, nd_acc), (gu_hbm, gd_hbm)

    loads = [pltpu.make_async_copy(ut_hbm, act, insem.at[0]), pltpu.make_async_copy(et_hbm, side, insem.at[1])]
    for c in loads:
        c.start()

    def wcopies(j, slot, back):
        second = w2_hbm if back else w4_hbm
        cps = [pltpu.make_async_copy(second.at[:, j], wb.at[slot], wsem.at[1, slot])]
        if not back:
            cps.append(pltpu.make_async_copy(w3_hbm.at[:, j], wa.at[slot], wsem.at[0, slot]))
        return cps
    for c in wcopies(0, 0, False):
        c.start()

    meet([partner] + [me + 2 * s for s in steps])

    nu[...] = jnp.zeros_like(nu)
    nd_acc[...] = jnp.zeros_like(nd_acc)
    gt[1] = jnp.zeros_like(gt[1])
    def zero(r, _):
        euacc[:, aligned(r, rb)] = jnp.zeros((d, rb), F32)
        return 0
    lax.fori_loop(0, nr, zero, 0)

    def send(kind, stage, j):
        depth = R[kind][stage].shape[0]
        slot = lax.rem(j, depth)
        sem = (kind * len(SEEN) + stage) * max(DEPTH) + slot
        dst = R[kind][stage].at[slot]
        if stage == 0:
            src, dev = G[kind].at[lax.rem(j, G[kind].shape[0]), :, 1 - core], partner
        else:
            lo = PARTS >> stage
            src, dev = ACC[kind][stage - 1].at[lax.rem(j, HOLD), pl.ds(lo, lo)], me + 2 * hop(steps, kind, stage - 1, j)
        return pltpu.make_async_remote_copy(src_ref=src, dst_ref=dst, send_sem=ssem.at[sem], recv_sem=rsem.at[sem],
                                            device_id=(dev,), device_id_type=MESH)

    def final_copy(kind, j):
        slot = lax.rem(j, 2)
        return pltpu.make_async_copy(FIN[kind].at[slot], OUT[kind].at[j], fsem.at[kind, slot])

    def absorb(stage, j):
        place = lax.rem(j, HOLD)
        for kind in range(2):
            send(kind, stage, j).wait()
            slot = lax.rem(j, R[kind][stage].shape[0])
            got, acc = R[kind][stage], ACC[kind]
            if stage == 0:
                hops = [hop(steps, kind, place, j) for place in range(AXES)]
                for p in range(PARTS):
                    oc = chip + relative(hops, p)
                    acc[0][place, p] = G[kind][lax.rem(j, G[kind].shape[0]), oc, core] + got[slot, oc]
                continue
            kept = acc[stage - 1][place, 0:PARTS >> stage] + got[slot]
            if stage < LAST:
                acc[stage][place] = kept
            else:
                @pl.when(j >= 2)
                def _():
                    final_copy(kind, j - 2).wait()
                f = kept[0] * (1.0 / nd)
                FIN[kind][lax.rem(j, 2)] = f
                NRM[kind][...] += f * f
        for kind in range(2):
            (send(kind, stage + 1, j) if stage < LAST else final_copy(kind, j)).start()

    def comm(step):
        def when_valid(j, fn):
            @pl.when(jnp.logical_and(j >= 0, j < total))
            def _():
                fn()
        for stage in reversed(range(len(SEEN))):
            when_valid(step - SEEN[stage], functools.partial(absorb, stage, step - SEEN[stage]))
        def start():
            for kind in range(2):
                send(kind, 0, step - BEGUN).start()
        when_valid(step - BEGUN, start)

    def turn(step, part):
        slot = lax.rem(step + 1, 2)
        lanes = pl.ds(part * TURN, TURN)
        gd[slot, :, :, :, lanes] = gt[slot, lanes, :].T.reshape(gd.shape[1:-1] + (TURN,))

    def add_up(step, r, value):
        slot, value = lax.rem(step, gu.shape[0]), value.reshape(gu.shape[1:])
        gu[slot] = value if r == 0 else gu[slot] + value

    def add_down(step, r, value):
        slot = lax.rem(step, 2)
        gt[slot] = value if r == 0 else gt[slot] + value

    def gates(r, width, pre):
        h, der = gelu_pair(pre)
        lanes = pl.ds(0, width)
        hb[r % 2][:, lanes] = h.astype(BF16)
        qb[r % 2][:, lanes] = (eb[r % 2][:, lanes].astype(F32) * der).astype(BF16)

    def pipeline(step, blocks, front, middle, back):
        front(0)
        for r in range(blocks):
            middle(r)
            if r + 1 < blocks:
                front(r + 1)
            if r >= 1:
                back(r - 1)
            for part in range(r, d // TURN, blocks):
                turn(step, part)
        back(blocks - 1)

    for c in loads:
        c.wait()

    def tile_b(j, _):
        slot = lax.rem(j, 2)
        comm(j)
        for c in wcopies(j, slot, False):
            c.wait()
        @pl.when(j + 1 < nt)
        def _():
            for c in wcopies(j + 1, 1 - slot, False):
                c.start()
        def cols(r):
            return pl.ds(r * rb, rb)
        mine = pl.ds(0, rb)
        def front(r):
            zb[r % 2][...] = dot_nn(wa[slot].reshape(ft, d), act[:, cols(r)])
            eb[r % 2][:, mine] = dot_nn(wb[slot].reshape(ft, d), side[:, cols(r)]).astype(BF16)
            if r == 0:
                wat[...] = wa[slot].reshape(ft, d).T
        def middle(r):
            gates(r, rb, zb[r % 2][...])
        def back(r):
            q = qb[r % 2][:, mine]
            add_up(j, r, dot_nt(act[:, cols(r)], q))
            add_down(j, r, dot_nt(side[:, cols(r)], hb[r % 2][:, mine]))
            euacc[:, cols(r)] += dot_nn(wat[...], q)
        pipeline(j, nr, front, middle, back)
        return 0
    lax.fori_loop(0, nt, tile_b, 0)

    xt_in = pltpu.make_async_copy(xt_hbm, side, insem.at[1])
    xt_in.start()
    for c in wcopies(0, nt % 2, True):
        c.start()
    def cast(r, _):
        act[:, aligned(r, rb)] = euacc[:, aligned(r, rb)].astype(BF16)
        return 0
    lax.fori_loop(0, nr, cast, 0)
    def zcopy(j, slot):
        return pltpu.make_async_copy(z_hbm.at[j], euacc.at[aligned(slot, ft), :], zsem.at[slot])
    zcopy(0, nt % 2).start()
    xt_in.wait()

    def tile_c(step, _):
        j = step - nt
        slot = lax.rem(step, 2)
        comm(step)
        for c in wcopies(j, slot, True):
            c.wait()
        zcopy(j, slot).wait()
        @pl.when(j + 1 < nt)
        def _():
            for c in wcopies(j + 1, 1 - slot, True):
                c.start()
            zcopy(j + 1, 1 - slot).start()
        def cols(r):
            return pl.ds(r * rc, rc)
        mine = pl.ds(0, rc)
        def front(r):
            eb[r % 2][:, mine] = dot_nn(wb[slot].reshape(ft, d), act[:, cols(r)]).astype(BF16)
        def middle(r):
            gates(r, rc, euacc[aligned(slot, ft), cols(r)])
        def back(r):
            add_down(step, r, dot_nt(act[:, cols(r)], hb[r % 2][:, mine]))
            add_up(step, r, dot_nt(side[:, cols(r)], qb[r % 2][:, mine]))
        pipeline(step, nc, front, middle, back)
        return 0
    lax.fori_loop(nt, total, tile_c, 0)

    def drain(step, _):
        comm(step)
        @pl.when(step == total)
        def _():
            for part in range(d // TURN):
                turn(step, part)
        return 0
    lax.fori_loop(total, total + SEEN[LAST], drain, 0)
    for kind in range(2):
        for j in (total - 2, total - 1):
            final_copy(kind, j).wait()

    part = jnp.zeros((8, 128), F32)
    for ref in (nu, nd_acc):
        rows, cols = ref.shape
        for a in range(rows // 8):
            for b in range(cols // 128):
                part = part + ref[8 * a:8 * a + 8, 128 * b:128 * b + 128]
    nrm_ref[...] = part


def backward(ut, et, xt, z, w3r, w4r, w2r):
    d, t = ut.shape
    nd, nt, rows2, _ = w4r.shape
    ft, nr, nc = nd * rows2, BACK_BLOCKS, BACK_BLOCKS // 2
    rb, rc = t // nr, t // nc
    bu, bd = (d // nd, ft), (rows2, d)
    V, D = pltpu.VMEM, pltpu.SemaphoreType.DMA
    S = jax.ShapeDtypeStruct
    scratch = [V((d, t), BF16)] * 2 + [V((d, t), F32)] + [V((2, nd, rows2, d), BF16)] * 2 + [V((d, ft), BF16)]
    scratch += [V((ft, rb), F32)] * 2 + [V((ft, rc), BF16)] * 6
    scratch += [V((3, PARTS, 2) + bu, F32), V((2, d, ft), F32), V((2, PARTS, 2) + bd, F32)]
    for n, c in [(DEPTH[0], PARTS)] + [(HOLD, PARTS >> k) for k in range(LAST)] + [(DEPTH[k], PARTS >> k) for k in range(1, LAST + 1)]:
        scratch += [V((n, c) + bu, F32), V((n, c) + bd, F32)]
    scratch += [V((2,) + bu, F32), V((2,) + bd, F32), V(bu, F32), V(bd, F32)]
    flags = 2 * len(SEEN) * max(DEPTH)
    scratch += [D((2,)), D((2, 2)), D((2,)), D((flags,)), D((flags,)), D((2, 2))]
    return pl.pallas_call(
        functools.partial(kernel_bc, (nt, nr, nc, t, ft, d, nd)),
        out_shape=(S((2 * nt,) + bu, F32), S((2 * nt,) + bd, F32), S((8, 128), F32)),
        in_specs=[HBM] * 7, out_specs=(HBM, HBM, pl.BlockSpec(memory_space=pltpu.VMEM)),
        scratch_shapes=scratch,
        compiler_params=pltpu.CompilerParams(collective_id=0, has_side_effects=True, vmem_limit_bytes=VMEM_MAX),
        name="backward",
    )(ut, et, xt, z, w3r, w4r, w2r)


STEP = 20
BETA_ONE = 0.9
BETA_TWO = 0.95
EPSILON = 1e-8
NORM_EPS = 1e-6
CORR_ONE = 1.0 - BETA_ONE ** STEP
CORR_TWO = 1.0 - BETA_TWO ** STEP
LANES = 128
WIDTH = 16
LAG = 2
AHEAD = 2
EMIT = 4
UPDATE_VMEM = 19 * 1024 * 1024 + 256 * 1024
EMIT_VMEM = 17 * 1024 * 1024


def clip_scale(norm, clip):
    return jnp.minimum(1.0, clip / (norm + NORM_EPS))


def adam_rows(scale, rate, grad, master, mom, vel):
    scaled = scale * grad
    mom = BETA_ONE * mom + (1.0 - BETA_ONE) * scaled
    vel = BETA_TWO * vel + (1.0 - BETA_TWO) * scaled * scaled
    master = master - rate * (mom * (1.0 / CORR_ONE)) / (jnp.sqrt(vel * (1.0 / CORR_TWO)) + EPSILON)
    return master, mom, vel


def natural_columns(gbuf, layer, first, count, nd, nt):
    rows, per = gbuf.shape[2], LANES // WIDTH
    group = lax.broadcasted_iota(jnp.int32, (rows, LANES), 1) // WIDTH
    tiles = []
    for t in range(count):
        acc = None
        for s in range(per):
            place = per * (first + t) + s
            owner, j = lax.div(place, nt), lax.rem(place, nt)
            src = gbuf[layer, j, :, aligned(lax.div(owner, per), LANES)]
            turned = pltpu.roll(src, lax.rem(s - lax.rem(owner, per) + per, per) * WIDTH, 1)
            acc = turned if acc is None else jnp.where(group == s, turned, acc)
        tiles.append(acc)
    return jnp.concatenate(tiles, axis=1)


def state_loads(gu_hbm, gd_hbm, states, gbuf, sbuf, sem):
    loads = []
    for kind, src in enumerate((gu_hbm, gd_hbm)):
        nt = src.shape[0] // 2
        for layer in range(2):
            loads.append(pltpu.make_async_copy(src.at[pl.ds((1 - layer) * nt, nt)], gbuf[kind].at[layer], sem.at[kind, layer, 3]))
            for f in range(3):
                loads.append(pltpu.make_async_copy(states[4 * f + 2 * layer + kind], sbuf[kind].at[layer, f], sem.at[kind, layer, f]))
    return loads


def kernel_update(cfg, part_ref, rate_ref, clip_ref, gu_hbm, gd_hbm, *refs):
    nd, pieces, ru, cu, rd = cfg
    states, (ou1, ou2, od1, od2, norm_ref), (su, sd, gbuf_u, gbuf_d, sbuf_u, sbuf_d, nrecv, insem, nsem, lsem, rsem, ssem, dsem) = refs[:12], refs[12:17], refs[17:]
    me, core, chip, steps = position()
    partner = flip(me, 1)
    IN, O = (su, sd), ((ou1, ou2), (od1, od2))
    layers = range(len(O[0]))
    loads = state_loads(gu_hbm, gd_hbm, states, (gbuf_u, gbuf_d), (sbuf_u, sbuf_d), insem)
    for c in loads:
        c.start()
    meet([lax.rem(me + k, nd) for k in range(1, nd)])
    nrecv[me] = part_ref[...]
    for k in range(1, nd):
        pltpu.make_async_remote_copy(src_ref=part_ref, dst_ref=nrecv.at[me], send_sem=nsem.at[0], recv_sem=nsem.at[1],
                                     device_id=(lax.rem(me + k, nd),), device_id_type=MESH).start()

    def block(kind, first, j, ref):
        if kind == 0:
            return ref.at[pl.ds(pl.multiple_of(first, 8), ru), aligned(j, cu)]
        return ref.at[pl.ds(pl.multiple_of(first + j * rd, 8), rd), :]

    height = (ru, rd * pieces)
    own = [pltpu.make_async_copy(IN[kind].at[w], O[kind][w].at[aligned(me, height[kind]), :], lsem.at[kind, w])
           for kind in range(2) for w in layers]

    def push(kind, p, j, hops, dev, send, recv):
        first = (2 * (chip + relative(hops, p)) + core) * height[kind]
        for w in layers:
            dst = block(kind, first, j, O[kind][w])
            src = dst if p else block(kind, 0, j, IN[kind].at[w])
            pltpu.make_async_remote_copy(src_ref=src, dst_ref=dst, send_sem=send, recv_sem=recv, device_id=(dev,), device_id_type=MESH).start()

    def flag(kind, stage, j):
        return rsem.at[kind, stage, lax.rem(j, AXES * LAG)]

    def spread(kind, stage, j, hops):
        dev = me + 2 * hops[AXES - 1 - stage]
        for p in range(1 << stage):
            push(kind, p, j, hops, dev, ssem.at[kind, stage], flag(kind, stage, j))

    def await_bytes(ref, sem, recv):
        cp = pltpu.make_async_remote_copy(src_ref=ref, dst_ref=ref, send_sem=sem, recv_sem=sem, device_id=(me,), device_id_type=MESH)
        if recv:
            cp.wait_recv()
        else:
            cp.wait_send()

    def arrived(kind, stage, j):
        n = 2 << stage
        part = O[kind][0].at[pl.ds(0, n * ru), pl.ds(0, cu)] if kind == 0 else O[kind][0].at[pl.ds(0, n * rd), :]
        await_bytes(part, flag(kind, stage, j), True)

    for c in loads:
        c.wait()
    others = nrecv.at[pl.ds(0, nd - 1)]
    await_bytes(others, nsem.at[0], False)
    await_bytes(others, nsem.at[1], True)
    total_sq = nrecv[0]
    for k in range(1, nd):
        total_sq = total_sq + nrecv[k]
    norm = jnp.sqrt(jnp.sum(total_sq, keepdims=True))
    norm_ref[...] = jnp.broadcast_to(norm, norm_ref.shape)
    rate, scale = rate_ref[0], clip_scale(norm, clip_ref[0])

    def make(j):
        for w in layers:
            cols = aligned(j, cu)
            grad = natural_columns(gbuf_u, w, j * (cu // LANES), cu // LANES, nd, pieces)
            old = [sbuf_u[w, f, :, cols] for f in range(3)]
            su[w, :, cols] = adam_rows(scale, rate, grad, *old)[0].astype(BF16)
            rows = aligned(j, rd)
            old = [sbuf_d[w, f, rows, :] for f in range(3)]
            sd[w, rows, :] = adam_rows(scale, rate, gbuf_d[w, j], *old)[0].astype(BF16)

    def step(s, _):
        for stage in reversed(range(AXES + 1)):
            j = s - stage * LAG
            @pl.when(jnp.logical_and(j >= 0, j < pieces))
            def _():
                for kind in range(2):
                    hops = [hop(steps, kind, place, j) for place in range(AXES)]
                    if stage:
                        arrived(kind, stage - 1, j)
                    if stage < AXES:
                        spread(kind, stage, j, hops)
                    for p in range((1 << stage) >> 1, 1 << stage):
                        push(kind, p, j, hops, partner, dsem.at[0, kind], dsem.at[1, kind])
        @pl.when(s + AHEAD < pieces)
        def _():
            make(s + AHEAD)
        return 0
    for j in range(AHEAD):
        make(j)
    lax.fori_loop(0, pieces + AXES * LAG, step, 0)
    for c in own:
        c.start()
    for c in own:
        c.wait()
    for kind in range(2):
        full = O[kind][0]
        await_bytes(full, dsem.at[0, kind], False)
        await_bytes(full, dsem.at[1, kind], True)
        for stage in range(AXES):
            await_bytes(full.at[pl.ds(0, (2 << stage) * height[kind]), :], ssem.at[kind, stage], False)


def update(part, rate, clip, gu, gd, states, nd):
    (ru, f), (rf, d) = states[0].shape, states[1].shape
    pieces = gd.shape[0] // 2
    V, D, S = pltpu.VMEM, pltpu.SemaphoreType.DMA, jax.ShapeDtypeStruct
    anyspec, vm, sm = [pl.BlockSpec(memory_space=m) for m in (pl.ANY, pltpu.VMEM, pltpu.SMEM)]
    return pl.pallas_call(
        functools.partial(kernel_update, (nd, pieces, ru, f // pieces, rf // pieces)),
        out_shape=(S((ru * nd, f), BF16),) * 2 + (S((rf * nd, d), BF16),) * 2 + (S((8, LANES), F32),),
        in_specs=[vm, sm, sm] + [HBM] * 14, out_specs=(anyspec,) * 4 + (vm,),
        scratch_shapes=[V((2, ru, f), BF16), V((2, rf, d), BF16), V((2, pieces) + gu.shape[1:], F32), V((2, pieces) + gd.shape[1:], F32),
                        V((2, 3, ru, f), F32), V((2, 3, rf, d), F32), V((nd, 8, LANES), F32),
                        D((2, 2, 4)), D((2,)), D((2, 2)), D((2, AXES, AXES * LAG)), D((2, AXES)), D((2, 2))],
        compiler_params=pltpu.CompilerParams(collective_id=1, has_side_effects=True, vmem_limit_bytes=UPDATE_VMEM),
        name="update")(part, rate, clip, gu, gd, *states)


def kernel_emit(cfg, norm_ref, rate_ref, clip_ref, gu_hbm, gd_hbm, *refs):
    nd, nt = cfg
    weights, states, refs = refs[:4], refs[4:16], refs[16:]
    weights_out, states_out, norm_out = refs[:4], refs[4:16], refs[16]
    gbuf_u, gbuf_d, sbuf_u, sbuf_d, insem, wsem, osem = refs[17:]
    gbuf, sbuf = (gbuf_u, gbuf_d), (sbuf_u, sbuf_d)
    loads = state_loads(gu_hbm, gd_hbm, states, gbuf, sbuf, insem)
    for c in loads:
        c.start()
    copies = []
    for k, (src, dst) in enumerate(zip(weights, weights_out)):
        rows = src.shape[0] // EMIT
        for part in range(EMIT):
            piece = pl.ds(part * rows, rows)
            copies.append(pltpu.make_async_copy(src.at[piece, :], dst.at[piece, :], wsem.at[k, part]))
    for c in copies:
        c.start()
    norm = norm_ref[0:1, 0:1]
    norm_out[...] = norm
    rate, scale = rate_ref[0], clip_scale(norm, clip_ref[0])
    for n, c in enumerate(loads):
        c.wait()
        kind, layer = n // 8, n // 4 % 2
        if n % 4 < 3:
            continue
        def renew(rows, cols, grad):
            old = [sbuf[kind][layer, f, rows, cols] for f in range(3)]
            for f, value in enumerate(adam_rows(scale, rate, grad, *old)):
                sbuf[kind][layer, f, rows, cols] = value
        def body(j, _):
            if kind == 0:
                wide = sbuf_u.shape[3] // nt
                renew(slice(None), aligned(j, wide), natural_columns(gbuf_u, layer, j * (wide // LANES), wide // LANES, nd, nt))
            else:
                renew(aligned(j, gbuf_d.shape[2]), slice(None), gbuf_d[layer, j])
            return 0
        lax.fori_loop(0, nt, body, 0)
        for f in range(3):
            cp = pltpu.make_async_copy(sbuf[kind].at[layer, f], states_out[4 * f + 2 * layer + kind], osem.at[kind, layer, f])
            cp.start()
            copies.append(cp)
    for c in copies:
        c.wait()


def emit(norm, rate, clip, gu, gd, weights, states, nd):
    nt = gu.shape[0] // 2
    up, down = states[0].shape, states[1].shape
    V, D, S = pltpu.VMEM, pltpu.SemaphoreType.DMA, jax.ShapeDtypeStruct
    anyspec, vm, sm = [pl.BlockSpec(memory_space=m) for m in (pl.ANY, pltpu.VMEM, pltpu.SMEM)]
    return pl.pallas_call(
        functools.partial(kernel_emit, (nd, nt)),
        out_shape=[S(a.shape, a.dtype) for a in (*weights, *states)] + [S((1, 1), F32)],
        in_specs=[vm, sm, sm] + [HBM] * 2 + [anyspec] * 4 + [HBM] * 12, out_specs=[HBM] * 16 + [vm],
        scratch_shapes=[V((2, nt) + gu.shape[1:], F32), V((2, nt) + gd.shape[1:], F32), V((2, 3) + up, F32), V((2, 3) + down, F32),
                        D((2, 2, 4)), D((4, EMIT)), D((2, 2, 3))],
        compiler_params=pltpu.CompilerParams(vmem_limit_bytes=EMIT_VMEM), name="emit")(norm, rate, clip, gu, gd, *weights, *states)


def solution(mesh):
    groups = mesh.shape["data"]
    rows_spec = P("data", None)
    full_spec = P(None, None)
    scalar_spec = P()

    def shard_body(act_in, grad_out, w_up1, w_down1, w_up2, w_down2, *rest):
        states, learn_rate, clip_norm = rest[:12], rest[12], rest[13]
        ff, d = w_down1.shape
        down1_tiles = w_down1.reshape(groups, -1, 16, d)
        down2_tiles = w_down2.reshape(groups, -1, 16, d)
        pre1, mid_t, in_t, grad_t, up2_t = forward_one(act_in, grad_out, w_up1, w_up2, down1_tiles)
        up2_tiles = up2_t.reshape(down1_tiles.shape)
        grads_up, grads_down, sq = backward(mid_t, grad_t, in_t, pre1, up2_tiles, down2_tiles, down1_tiles)
        rate, clip = learn_rate.reshape(1), clip_norm.reshape(1)
        states = [pltpu.with_memory_space_constraint(x, pltpu.HBM) for x in states]
        grads_up, grads_down = [pltpu.with_memory_space_constraint(x, pltpu.HBM) for x in (grads_up, grads_down)]
        up1, up2, down1, down2, norm = update(sq, rate, clip, grads_up, grads_down, states, groups)
        *results, norm = emit(norm, rate, clip, grads_up, grads_down, (up1, down1, up2, down2), states, groups)
        return (*results, norm.reshape(()))

    in_specs = (rows_spec, rows_spec) + (full_spec,) * 4 + (rows_spec,) * 12 + (scalar_spec, scalar_spec)
    out_specs = (full_spec,) * 4 + (rows_spec,) * 12 + (scalar_spec,)
    return jax.shard_map(shard_body, mesh=mesh, in_specs=in_specs, out_specs=out_specs, check_vma=False)
```

profile of v0, /device:TPU:0, one launch (start us, length us, event | category | flops | bytes accessed | tf_op | source)
XLA Modules:
  0.0 625.4 jit_solution(2951055030102868397)
XLA Ops:
  0.7 100.9 %forward_one.1 = (f32[19,256,4096]{2,1,0:T(8,128)}, bf16[896,4096]{1,0:T(8,128)(2,1)}, bf16[896,4096]{1,0:T(8,128)(2,1)}, bf16[896,4096]{1,0:T(8,128)(2,1)}, bf16[4864,896]{1,0:T(8,128)(2,1)}) custom-call(bf16[4096,896]{1,0:T(8,128)(2,1)} %x_hbm.1, bf16[4096,896]{1,0:T(8,128)(2,1)} %e_hbm.1, bf16[896,4864]{1,0:T(8,128)(2,1)} %w1_hbm.1, ...), custom_call_target="tpu_custom_call" | custom-call | tf_op jit(solution)/shard_map/forward_one/pallas_call | solution.py:198
  101.5 373.1 %backward.1 = (f32[38,56,256]{2,1,0:T(8,128)}, f32[38,16,896]{2,1,0:T(8,128)}, f32[8,128]{1,0:T(8,128)}) custom-call(bf16[896,4096]{1,0:T(8,128)(2,1)} %get-tuple-element.47.ut_hbm, bf16[896,4096]{1,0:T(8,128)(2,1)} %get-tuple-element.48.et_hbm, bf16[896,4096]{1,0:T(8,128)(2,1)} %get-tuple-element.49.xt_hbm, f32[19,256,4096]{2,1,0:T(8,128)} %get-tuple-element.50.z_hbm, ...), custom_call_target="tpu_custom_call" | custom-call | tf_op jit(solution)/shard_map/backward/pallas_call | solution.py:486
  476.0 0.0 copy-start
  476.0 0.7 copy-done
  476.6 126.8 %update.1 = (bf16[896,4864]{1,0:T(8,128)(2,1)S(1)}, bf16[896,4864]{1,0:T(8,128)(2,1)S(1)}, bf16[4864,896]{1,0:T(8,128)(2,1)S(1)}, bf16[4864,896]{1,0:T(8,128)(2,1)S(1)}, f32[8,128]{1,0:T(8,128)S(1)}) custom-call(f32[8,128]{1,0:T(8,128)S(1)} %copy-done, f32[1]{0:T(128)} %bitcast.6.rate_ref, f32[1]{0:T(128)} %bitcast.8.clip_ref, ...), custom_call_target="tpu_custom_call" | custom-call | tf_op jit(solution)/shard_map/update/pallas_call | solution.py:662
  603.5 21.7 %emit.1 = (bf16[896,4864]{1,0:T(8,128)(2,1)}, bf16[4864,896]{1,0:T(8,128)(2,1)}, bf16[896,4864]{1,0:T(8,128)(2,1)}, bf16[4864,896]{1,0:T(8,128)(2,1)}, f32[56,48...) custom-call(f32[8,128]{1,0:T(8,128)S(1)} %get-tuple-element.55.norm_, ...), custom_call_target="tpu_custom_call" | custom-call | tf_op jit(solution)/shard_map/emit/pallas_call | solution.py:723
Async XLA Ops:
  476.0 0.7 copy-start
where the time goes:
time: 626 us; the launch traced here: 625 us
  Pallas kernels  623 us (100%)
    pallas_call x1, Pallas kernels, backward(): pl.pallas_call(functools.partial(kernel_bc, (nt, nr, nc, t, ft, d, nd)),...  373 us
    pallas_call x1, Pallas kernels, update(): pl.pallas_call(functools.partial(kernel_update, (nd, pieces, ru, f // pie...  127 us
    pallas_call x1, Pallas kernels, forward_one(): pl.pallas_call(functools.partial(kernel_a, (nt, nr, rb, tr, tb, ft, d, nd...  101 us
    pallas_call x1, Pallas kernels, emit(): pl.pallas_call(functools.partial(kernel_emit, (nd, nt)), out_shape=[S(a.s...  21.7 us

commit v1 on v0

--- a/solution.py
+++ b/solution.py
@@ -12,9 +12,11 @@
 F32, BF16 = jnp.float32, jnp.bfloat16
 HBM = pl.BlockSpec(memory_space=pltpu.HBM)
 VMEM_MAX = 64 * 1024 * 1024 - 65536
+PAIR = 2
 BLOCKS = 8
 TURNS = 8
-RING = 6
+RING = 4
+LANES = 128
 
 
 def dot_nn(a, b):
@@ -46,7 +48,7 @@
 
     def w1copy(q):
         slot = lax.rem(q, RING)
-        return pltpu.make_async_copy(w1_hbm.at[:, aligned(q, ft)], w1_in.at[slot], wsem.at[slot])
+        return pltpu.make_async_copy(w1_hbm.at[aligned(q, LANES), :], w1_in.at[slot], wsem.at[slot])
 
     def xcopy(r):
         slot = lax.rem(r, RING)
@@ -76,7 +78,8 @@
         slot = lax.rem(j, 2)
         return pltpu.make_async_copy(zout.at[slot], z_hbm.at[j], zsem.at[slot])
 
-    for q in range(min(RING, nt)):
+    rows_in = d // LANES
+    for q in range(min(RING, rows_in)):
         w1copy(q).start()
     for r in range(min(RING, tr)):
         xcopy(r).start()
@@ -88,23 +91,21 @@
         return 0
     lax.fori_loop(0, nr, zero, 0)
 
-    def turn_w1(q, _):
-        w1copy(q).wait()
-        w1t_v[aligned(q, ft), :] = w1_in[lax.rem(q, RING)].T
-        @pl.when(q + RING < nt)
+    def turn_in(q, _):
+        @pl.when(q < rows_in)
+        def _():
+            w1copy(q).wait()
+            w1t_v[:, aligned(q, LANES)] = w1_in[lax.rem(q, RING)].T
+        @pl.when(q + RING < rows_in)
         def _():
             w1copy(q + RING).start()
-        return 0
-    lax.fori_loop(0, nt, turn_w1, 0)
-
-    def turn_x(r, _):
-        xcopy(r).wait()
-        xt[:, aligned(r, tb)] = x_in[lax.rem(r, RING)].T
-        @pl.when(r + RING < tr)
-        def _():
-            xcopy(r + RING).start()
-        return 0
-    lax.fori_loop(0, tr, turn_x, 0)
+        xcopy(q).wait()
+        xt[:, aligned(q, tb)] = x_in[lax.rem(q, RING)].T
+        @pl.when(q + RING < tr)
+        def _():
+            xcopy(q + RING).start()
+        return 0
+    lax.fori_loop(0, tr, turn_in, 0)
     xt_store = pltpu.make_async_copy(xt, xt_hbm, osem.at[2, 0])
     xt_store.start()
 
@@ -169,11 +170,12 @@
     xt_store.wait()
 
     def finish(r, _):
-        xt[:, aligned(r, rb)] = uacc[:, aligned(r, rb)].astype(BF16)
+        block = aligned(r, rb)
+        xt[:, block] = uacc[:, block].astype(BF16)
+        pltpu.make_async_copy(xt.at[:, block], ut_hbm.at[:, block], osem.at[2, 1]).start()
         return 0
     lax.fori_loop(0, nr, finish, 0)
     ut_store = pltpu.make_async_copy(xt, ut_hbm, osem.at[2, 1])
-    ut_store.start()
     for j in (nt - 2, nt - 1):
         zstore(j).wait()
         w3store(j).wait()
@@ -200,10 +202,10 @@
         out_shape=(S((nt, ft, t), F32), S((d, t), BF16), S((d, t), BF16), S((d, t), BF16), S((nt * ft, d), BF16)),
         in_specs=[HBM] * 5, out_specs=(HBM,) * 5,
         scratch_shapes=[
-            V((d, t), BF16), V((d, t), F32), V((2, ft, t), F32), V((nt * ft, d), BF16), V((RING, d, ft), BF16), V((RING, tb, d), BF16),
-            V((2, ft, d), BF16), V((2, nd, rows2, d), BF16), V((d, ft), BF16), V((2, d, ft), BF16), V((2, ft, d), BF16),
-            V((2, tb, d), BF16), V((2, d, tb), BF16), V((ft, rb), BF16), V((ft, rb), BF16),
-            D((RING,)), D((RING,)), D((2,)), D((2, 2)), D((2,)), D((3, 2))],
+            V((d, t), BF16), V((d, t), F32), V((PAIR, ft, t), F32), V((nt * ft, d), BF16), V((RING, LANES, nt * ft), BF16), V((RING, tb, d), BF16),
+            V((PAIR, ft, d), BF16), V((PAIR, nd, rows2, d), BF16), V((d, ft), BF16), V((PAIR, d, ft), BF16), V((PAIR, ft, d), BF16),
+            V((PAIR, tb, d), BF16), V((PAIR, d, tb), BF16), V((ft, rb), BF16), V((ft, rb), BF16),
+            D((RING,)), D((RING,)), D((PAIR,)), D((PAIR, PAIR)), D((PAIR,)), D((3, 2))],
         compiler_params=pltpu.CompilerParams(vmem_limit_bytes=VMEM_MAX),
         name="forward_one",
     )(x, e, w1, w3, w2r)
@@ -236,6 +238,10 @@
 
 
 AXES = 3
+
+
+def when(condition, fn):
+    pl.when(condition)(fn)
 
 
 def meet(peers):
@@ -324,9 +330,7 @@
             if stage < LAST:
                 acc[stage][place] = kept
             else:
-                @pl.when(j >= 2)
-                def _():
-                    final_copy(kind, j - 2).wait()
+                when(j >= 2, final_copy(kind, j - 2).wait)
                 f = kept[0] * (1.0 / nd)
                 FIN[kind][lax.rem(j, 2)] = f
                 NRM[kind][...] += f * f
@@ -334,16 +338,15 @@
             (send(kind, stage + 1, j) if stage < LAST else final_copy(kind, j)).start()
 
     def comm(step):
-        def when_valid(j, fn):
-            @pl.when(jnp.logical_and(j >= 0, j < total))
-            def _():
-                fn()
+        def due(j, fn):
+            when(jnp.logical_and(j >= 0, j < total), fn)
         for stage in reversed(range(len(SEEN))):
-            when_valid(step - SEEN[stage], functools.partial(absorb, stage, step - SEEN[stage]))
+            j = step - SEEN[stage]
+            due(j, functools.partial(absorb, stage, j))
         def start():
             for kind in range(2):
                 send(kind, 0, step - BEGUN).start()
-        when_valid(step - BEGUN, start)
+        due(step - BEGUN, start)
 
     def turn(step, part):
         slot = lax.rem(step + 1, 2)
@@ -475,14 +478,14 @@
     bu, bd = (d // nd, ft), (rows2, d)
     V, D = pltpu.VMEM, pltpu.SemaphoreType.DMA
     S = jax.ShapeDtypeStruct
-    scratch = [V((d, t), BF16)] * 2 + [V((d, t), F32)] + [V((2, nd, rows2, d), BF16)] * 2 + [V((d, ft), BF16)]
+    scratch = [V((d, t), BF16)] * 2 + [V((d, t), F32)] + [V((PAIR, nd, rows2, d), BF16)] * 2 + [V((d, ft), BF16)]
     scratch += [V((ft, rb), F32)] * 2 + [V((ft, rc), BF16)] * 6
-    scratch += [V((3, PARTS, 2) + bu, F32), V((2, d, ft), F32), V((2, PARTS, 2) + bd, F32)]
+    scratch += [V((3, PARTS, 2) + bu, F32), V((PAIR, d, ft), F32), V((PAIR, PARTS, 2) + bd, F32)]
     for n, c in [(DEPTH[0], PARTS)] + [(HOLD, PARTS >> k) for k in range(LAST)] + [(DEPTH[k], PARTS >> k) for k in range(1, LAST + 1)]:
         scratch += [V((n, c) + bu, F32), V((n, c) + bd, F32)]
-    scratch += [V((2,) + bu, F32), V((2,) + bd, F32), V(bu, F32), V(bd, F32)]
+    scratch += [V((PAIR,) + bu, F32), V((PAIR,) + bd, F32), V(bu, F32), V(bd, F32)]
     flags = 2 * len(SEEN) * max(DEPTH)
-    scratch += [D((2,)), D((2, 2)), D((2,)), D((flags,)), D((flags,)), D((2, 2))]
+    scratch += [D((PAIR,)), D((PAIR, PAIR)), D((PAIR,)), D((flags,)), D((flags,)), D((PAIR, PAIR))]
     return pl.pallas_call(
         functools.partial(kernel_bc, (nt, nr, nc, t, ft, d, nd)),
         out_shape=(S((2 * nt,) + bu, F32), S((2 * nt,) + bd, F32), S((8, 128), F32)),
@@ -500,7 +503,6 @@
 NORM_EPS = 1e-6
 CORR_ONE = 1.0 - BETA_ONE ** STEP
 CORR_TWO = 1.0 - BETA_TWO ** STEP
-LANES = 128
 WIDTH = 16
 LAG = 2
 AHEAD = 2
@@ -537,31 +539,38 @@
     return jnp.concatenate(tiles, axis=1)
 
 
-def state_loads(gu_hbm, gd_hbm, states, gbuf, sbuf, sem):
+def state_loads(gu_hbm, gd_hbm, states, gbuf, sbuf, sem, lo, hi):
     loads = []
     for kind, src in enumerate((gu_hbm, gd_hbm)):
-        nt = src.shape[0] // 2
+        nt, size = src.shape[0] // 2, src.shape[2] if kind == 0 else src.shape[1]
+        part = pl.ds(lo * size, (hi - lo) * size)
         for layer in range(2):
-            loads.append(pltpu.make_async_copy(src.at[pl.ds((1 - layer) * nt, nt)], gbuf[kind].at[layer], sem.at[kind, layer, 3]))
+            first, count = (lo, hi - lo) if kind else (0, nt if lo == 0 else 0)
+            if count:
+                loads.append(pltpu.make_async_copy(src.at[pl.ds((1 - layer) * nt + first, count)], gbuf[kind].at[layer, pl.ds(first, count)],
+                                                   sem.at[kind, layer, 3]))
             for f in range(3):
-                loads.append(pltpu.make_async_copy(states[4 * f + 2 * layer + kind], sbuf[kind].at[layer, f], sem.at[kind, layer, f]))
+                whole, mine = states[4 * f + 2 * layer + kind], sbuf[kind].at[layer, f]
+                pair = (whole.at[:, part], mine.at[:, part]) if kind == 0 else (whole.at[part, :], mine.at[part, :])
+                loads.append(pltpu.make_async_copy(*pair, sem.at[kind, layer, f]))
     return loads
 
 
-def kernel_update(cfg, part_ref, rate_ref, clip_ref, gu_hbm, gd_hbm, *refs):
+def kernel_update(cfg, part_hbm, rate_ref, clip_ref, gu_hbm, gd_hbm, *refs):
     nd, pieces, ru, cu, rd = cfg
     states, (ou1, ou2, od1, od2, norm_ref), (su, sd, gbuf_u, gbuf_d, sbuf_u, sbuf_d, nrecv, insem, nsem, lsem, rsem, ssem, dsem) = refs[:12], refs[12:17], refs[17:]
     me, core, chip, steps = position()
     partner = flip(me, 1)
     IN, O = (su, sd), ((ou1, ou2), (od1, od2))
     layers = range(len(O[0]))
-    loads = state_loads(gu_hbm, gd_hbm, states, (gbuf_u, gbuf_d), (sbuf_u, sbuf_d), insem)
-    for c in loads:
+    loads = [state_loads(gu_hbm, gd_hbm, states, (gbuf_u, gbuf_d), (sbuf_u, sbuf_d), insem.at[n], *span)
+             for n, span in enumerate(((0, AHEAD), (AHEAD, pieces)))]
+    keep = pltpu.make_async_copy(part_hbm, nrecv.at[me], nsem.at[2])
+    for c in (keep, *loads[0], *loads[1]):
         c.start()
     meet([lax.rem(me + k, nd) for k in range(1, nd)])
-    nrecv[me] = part_ref[...]
     for k in range(1, nd):
-        pltpu.make_async_remote_copy(src_ref=part_ref, dst_ref=nrecv.at[me], send_sem=nsem.at[0], recv_sem=nsem.at[1],
+        pltpu.make_async_remote_copy(src_ref=part_hbm, dst_ref=nrecv.at[me], send_sem=nsem.at[0], recv_sem=nsem.at[1],
                                      device_id=(lax.rem(me + k, nd),), device_id_type=MESH).start()
 
     def block(kind, first, j, ref):
@@ -600,8 +609,7 @@
         part = O[kind][0].at[pl.ds(0, n * ru), pl.ds(0, cu)] if kind == 0 else O[kind][0].at[pl.ds(0, n * rd), :]
         await_bytes(part, flag(kind, stage, j), True)
 
-    for c in loads:
-        c.wait()
+    keep.wait()
     others = nrecv.at[pl.ds(0, nd - 1)]
     await_bytes(others, nsem.at[0], False)
     await_bytes(others, nsem.at[1], True)
@@ -639,8 +647,12 @@
         def _():
             make(s + AHEAD)
         return 0
+    for c in loads[0]:
+        c.wait()
     for j in range(AHEAD):
         make(j)
+    for c in loads[1]:
+        c.wait()
     lax.fori_loop(0, pieces + AXES * LAG, step, 0)
     for c in own:
         c.start()
@@ -662,10 +674,10 @@
     return pl.pallas_call(
         functools.partial(kernel_update, (nd, pieces, ru, f // pieces, rf // pieces)),
         out_shape=(S((ru * nd, f), BF16),) * 2 + (S((rf * nd, d), BF16),) * 2 + (S((8, LANES), F32),),
-        in_specs=[vm, sm, sm] + [HBM] * 14, out_specs=(anyspec,) * 4 + (vm,),
-        scratch_shapes=[V((2, ru, f), BF16), V((2, rf, d), BF16), V((2, pieces) + gu.shape[1:], F32), V((2, pieces) + gd.shape[1:], F32),
-                        V((2, 3, ru, f), F32), V((2, 3, rf, d), F32), V((nd, 8, LANES), F32),
-                        D((2, 2, 4)), D((2,)), D((2, 2)), D((2, AXES, AXES * LAG)), D((2, AXES)), D((2, 2))],
+        in_specs=[HBM, sm, sm] + [HBM] * 14, out_specs=(anyspec,) * 4 + (vm,),
+        scratch_shapes=[V((PAIR, ru, f), BF16), V((PAIR, rf, d), BF16), V((PAIR, pieces) + gu.shape[1:], F32), V((PAIR, pieces) + gd.shape[1:], F32),
+                        V((PAIR, 3, ru, f), F32), V((PAIR, 3, rf, d), F32), V((nd, 8, LANES), F32),
+                        D((2, 2, 2, 4)), D((3,)), D((PAIR, PAIR)), D((2, AXES, AXES * LAG)), D((2, AXES)), D((PAIR, PAIR))],
         compiler_params=pltpu.CompilerParams(collective_id=1, has_side_effects=True, vmem_limit_bytes=UPDATE_VMEM),
         name="update")(part, rate, clip, gu, gd, *states)
 
@@ -676,7 +688,7 @@
     weights_out, states_out, norm_out = refs[:4], refs[4:16], refs[16]
     gbuf_u, gbuf_d, sbuf_u, sbuf_d, insem, wsem, osem = refs[17:]
     gbuf, sbuf = (gbuf_u, gbuf_d), (sbuf_u, sbuf_d)
-    loads = state_loads(gu_hbm, gd_hbm, states, gbuf, sbuf, insem)
+    loads = state_loads(gu_hbm, gd_hbm, states, gbuf, sbuf, insem, 0, nt)
     for c in loads:
         c.start()
     copies = []
@@ -724,7 +736,7 @@
         functools.partial(kernel_emit, (nd, nt)),
         out_shape=[S(a.shape, a.dtype) for a in (*weights, *states)] + [S((1, 1), F32)],
         in_specs=[vm, sm, sm] + [HBM] * 2 + [anyspec] * 4 + [HBM] * 12, out_specs=[HBM] * 16 + [vm],
-        scratch_shapes=[V((2, nt) + gu.shape[1:], F32), V((2, nt) + gd.shape[1:], F32), V((2, 3) + up, F32), V((2, 3) + down, F32),
+        scratch_shapes=[V((PAIR, nt) + gu.shape[1:], F32), V((PAIR, nt) + gd.shape[1:], F32), V((PAIR, 3) + up, F32), V((PAIR, 3) + down, F32),
                         D((2, 2, 4)), D((4, EMIT)), D((2, 2, 3))],
         compiler_params=pltpu.CompilerParams(vmem_limit_bytes=EMIT_VMEM), name="emit")(norm, rate, clip, gu, gd, *weights, *states)
 
@@ -745,7 +757,7 @@
         grads_up, grads_down, sq = backward(mid_t, grad_t, in_t, pre1, up2_tiles, down2_tiles, down1_tiles)
         rate, clip = learn_rate.reshape(1), clip_norm.reshape(1)
         states = [pltpu.with_memory_space_constraint(x, pltpu.HBM) for x in states]
-        grads_up, grads_down = [pltpu.with_memory_space_constraint(x, pltpu.HBM) for x in (grads_up, grads_down)]
+        sq, grads_up, grads_down = [pltpu.with_memory_space_constraint(x, pltpu.HBM) for x in (sq, grads_up, grads_down)]
         up1, up2, down1, down2, norm = update(sq, rate, clip, grads_up, grads_down, states, groups)
         *results, norm = emit(norm, rate, clip, grads_up, grads_down, (up1, down1, up2, down2), states, groups)
         return (*results, norm.reshape(()))

time: 626 us -> 623 us (level)
  no operation moved by 1% of the time
where the time goes in v1:
time: 623 us; the launch traced here: 622 us
  Pallas kernels  620 us (100%)
    pallas_call x1, Pallas kernels, backward(): pl.pallas_call(functools.partial(kernel_bc, (nt, nr, nc, t, ft, d, nd)),...  373 us
    pallas_call x1, Pallas kernels, update(): pl.pallas_call(functools.partial(kernel_update, (nd, pieces, ru, f // pie...  127 us
    pallas_call x1, Pallas kernels, forward_one(): pl.pallas_call(functools.partial(kernel_a, (nt, nr, rb, tr, tb, ft, d, nd...  98.2 us
    pallas_call x1, Pallas kernels, emit(): pl.pallas_call(functools.partial(kernel_emit, (nd, nt)), out_shape=[S(a.s...  21.7 us

profile of v1, /device:TPU:0, one launch (start us, length us, event | category | flops | bytes accessed | tf_op | source)
XLA Modules:
  0.0 621.9 jit_solution(16796679267668341484)
XLA Ops:
  0.7 98.2 %forward_one.1 = (f32[19,256,4096]{2,1,0:T(8,128)}, bf16[896,4096]{1,0:T(8,128)(2,1)}, bf16[896,4096]{1,0:T(8,128)(2,1)}, bf16[896,4096]{1,0:T(8,128)(2,1)}, bf16[4864,896]{1,0:T(8,128)(2,1)}) custom-call(bf16[4096,896]{1,0:T(8,128)(2,1)} %x_hbm.1, bf16[4096,896]{1,0:T(8,128)(2,1)} %e_hbm.1, bf16[896,4864]{1,0:T(8,128)(2,1)} %w1_hbm.1, ...), custom_call_target="tpu_custom_call" | custom-call | tf_op jit(solution)/shard_map/forward_one/pallas_call | solution.py:200
  98.9 373.1 %backward.1 = (f32[38,56,256]{2,1,0:T(8,128)}, f32[38,16,896]{2,1,0:T(8,128)}, f32[8,128]{1,0:T(8,128)}) custom-call(bf16[896,4096]{1,0:T(8,128)(2,1)} %get-tuple-element.47.ut_hbm, bf16[896,4096]{1,0:T(8,128)(2,1)} %get-tuple-element.48.et_hbm, bf16[896,4096]{1,0:T(8,128)(2,1)} %get-tuple-element.49.xt_hbm, f32[19,256,4096]{2,1,0:T(8,128)} %get-tuple-element.50.z_hbm, ...), custom_call_target="tpu_custom_call" | custom-call | tf_op jit(solution)/shard_map/backward/pallas_call | solution.py:489
  473.3 126.7 %update.1 = (bf16[896,4864]{1,0:T(8,128)(2,1)S(1)}, bf16[896,4864]{1,0:T(8,128)(2,1)S(1)}, bf16[4864,896]{1,0:T(8,128)(2,1)S(1)}, bf16[4864,896]{1,0:T(8,128)(2,1)S(1)}, f32[8,128]{1,0:T(8,128)S(1)}) custom-call(f32[8,128]{1,0:T(8,128)} %get-tuple-element.52.part_hbm, f32[1]{0:T(128)} %bitcast.6.rate_ref, f32[1]{0:T(128)} %bitcast.8.clip_ref, ...), custom_call_target="tpu_custom_call" | custom-call | tf_op jit(solution)/shard_map/update/pallas_call | solution.py:674
  600.0 21.7 %emit.1 = (bf16[896,4864]{1,0:T(8,128)(2,1)}, bf16[4864,896]{1,0:T(8,128)(2,1)}, bf16[896,4864]{1,0:T(8,128)(2,1)}, bf16[4864,896]{1,0:T(8,128)(2,1)}, f32[56,48...) custom-call(f32[8,128]{1,0:T(8,128)S(1)} %get-tuple-element.55.norm_, ...), custom_call_target="tpu_custom_call" | custom-call | tf_op jit(solution)/shard_map/emit/pallas_call | solution.py:735

commit v2 on v1

--- a/solution.py
+++ b/solution.py
@@ -414,13 +414,15 @@
     xt_in.start()
     for c in wcopies(0, nt % 2, True):
         c.start()
-    def cast(r, _):
-        act[:, aligned(r, rb)] = euacc[:, aligned(r, rb)].astype(BF16)
-        return 0
-    lax.fori_loop(0, nr, cast, 0)
     def zcopy(j, slot):
         return pltpu.make_async_copy(z_hbm.at[j], euacc.at[aligned(slot, ft), :], zsem.at[slot])
+    def cast(q, _):
+        rows = aligned(lax.rem(q + ft // TURN, d // TURN), TURN)
+        act[rows, :] = euacc[rows, :].astype(BF16)
+        return 0
+    lax.fori_loop(0, ft // TURN, cast, 0)
     zcopy(0, nt % 2).start()
+    lax.fori_loop(ft // TURN, d // TURN, cast, 0)
     xt_in.wait()
 
     def tile_c(step, _):
@@ -504,7 +506,7 @@
 CORR_ONE = 1.0 - BETA_ONE ** STEP
 CORR_TWO = 1.0 - BETA_TWO ** STEP
 WIDTH = 16
-LAG = 2
+LAG = 3
 AHEAD = 2
 EMIT = 4
 UPDATE_VMEM = 19 * 1024 * 1024 + 256 * 1024

time: 623 us -> 617 us (level)
  no operation moved by 1% of the time
where the time goes in v2:
time: 617 us; the launch traced here: 616 us
  Pallas kernels  614 us (100%)
    pallas_call x1, Pallas kernels, backward(): pl.pallas_call(functools.partial(kernel_bc, (nt, nr, nc, t, ft, d, nd)),...  373 us
    pallas_call x1, Pallas kernels, update(): pl.pallas_call(functools.partial(kernel_update, (nd, pieces, ru, f // pie...  121 us
    pallas_call x1, Pallas kernels, forward_one(): pl.pallas_call(functools.partial(kernel_a, (nt, nr, rb, tr, tb, ft, d, nd...  98.2 us
    pallas_call x1, Pallas kernels, emit(): pl.pallas_call(functools.partial(kernel_emit, (nd, nt)), out_shape=[S(a.s...  21.7 us

profile of v2, /device:TPU:0, one launch (start us, length us, event | category | flops | bytes accessed | tf_op | source)
XLA Modules:
  0.0 616.1 jit_solution(17210542798529064657)
XLA Ops:
  0.7 98.2 %forward_one.1 = (f32[19,256,4096]{2,1,0:T(8,128)}, bf16[896,4096]{1,0:T(8,128)(2,1)}, bf16[896,4096]{1,0:T(8,128)(2,1)}, bf16[896,4096]{1,0:T(8,128)(2,1)}, bf16[4864,896]{1,0:T(8,128)(2,1)}) custom-call(bf16[4096,896]{1,0:T(8,128)(2,1)} %x_hbm.1, bf16[4096,896]{1,0:T(8,128)(2,1)} %e_hbm.1, bf16[896,4864]{1,0:T(8,128)(2,1)} %w1_hbm.1, ...), custom_call_target="tpu_custom_call" | custom-call | tf_op jit(solution)/shard_map/forward_one/pallas_call | solution.py:200
  98.9 373.0 %backward.1 = (f32[38,56,256]{2,1,0:T(8,128)}, f32[38,16,896]{2,1,0:T(8,128)}, f32[8,128]{1,0:T(8,128)}) custom-call(bf16[896,4096]{1,0:T(8,128)(2,1)} %get-tuple-element.47.ut_hbm, bf16[896,4096]{1,0:T(8,128)(2,1)} %get-tuple-element.48.et_hbm, bf16[896,4096]{1,0:T(8,128)(2,1)} %get-tuple-element.49.xt_hbm, f32[19,256,4096]{2,1,0:T(8,128)} %get-tuple-element.50.z_hbm, ...), custom_call_target="tpu_custom_call" | custom-call | tf_op jit(solution)/shard_map/backward/pallas_call | solution.py:491
  473.2 121.1 %update.1 = (bf16[896,4864]{1,0:T(8,128)(2,1)S(1)}, bf16[896,4864]{1,0:T(8,128)(2,1)S(1)}, bf16[4864,896]{1,0:T(8,128)(2,1)S(1)}, bf16[4864,896]{1,0:T(8,128)(2,1)S(1)}, f32[8,128]{1,0:T(8,128)S(1)}) custom-call(f32[8,128]{1,0:T(8,128)} %get-tuple-element.52.part_hbm, f32[1]{0:T(128)} %bitcast.6.rate_ref, f32[1]{0:T(128)} %bitcast.8.clip_ref, ...), custom_call_target="tpu_custom_call" | custom-call | tf_op jit(solution)/shard_map/update/pallas_call | solution.py:676
  594.3 21.7 %emit.1 = (bf16[896,4864]{1,0:T(8,128)(2,1)}, bf16[4864,896]{1,0:T(8,128)(2,1)}, bf16[896,4864]{1,0:T(8,128)(2,1)}, bf16[4864,896]{1,0:T(8,128)(2,1)}, f32[56,48...) custom-call(f32[8,128]{1,0:T(8,128)S(1)} %get-tuple-element.55.norm_, ...), custom_call_target="tpu_custom_call" | custom-call | tf_op jit(solution)/shard_map/emit/pallas_call | solution.py:737

commit v3 on v2

--- a/solution.py
+++ b/solution.py
@@ -280,9 +280,9 @@
 
     def wcopies(j, slot, back):
         second = w2_hbm if back else w4_hbm
-        cps = [pltpu.make_async_copy(second.at[:, j], wb.at[slot], wsem.at[1, slot])]
+        cps = [pltpu.make_async_copy(second.at[:, j], wb.at[slot], wsem.at[slot])]
         if not back:
-            cps.append(pltpu.make_async_copy(w3_hbm.at[:, j], wa.at[slot], wsem.at[0, slot]))
+            cps.append(pltpu.make_async_copy(w3_hbm.at[:, j], wa.at[slot], wsem.at[slot]))
         return cps
     for c in wcopies(0, 0, False):
         c.start()
@@ -297,10 +297,20 @@
         return 0
     lax.fori_loop(0, nr, zero, 0)
 
+    def flag_of(stage, j):
+        return stage * max(DEPTH) + lax.rem(j, DEPTH[stage])
+
+    both = (gu.at[0], r0u.at[0], r1u.at[0], r2u.at[0])
+
+    def join(stage, j):
+        sem = flag_of(stage, j)
+        pltpu.make_async_remote_copy(src_ref=both[stage], dst_ref=both[stage], send_sem=ssem.at[sem], recv_sem=rsem.at[sem],
+                                     device_id=(me,), device_id_type=MESH).wait()
+
     def send(kind, stage, j):
         depth = R[kind][stage].shape[0]
         slot = lax.rem(j, depth)
-        sem = (kind * len(SEEN) + stage) * max(DEPTH) + slot
+        sem = flag_of(stage, j)
         dst = R[kind][stage].at[slot]
         if stage == 0:
             src, dev = G[kind].at[lax.rem(j, G[kind].shape[0]), :, 1 - core], partner
@@ -316,8 +326,8 @@
 
     def absorb(stage, j):
         place = lax.rem(j, HOLD)
+        join(stage, j)
         for kind in range(2):
-            send(kind, stage, j).wait()
             slot = lax.rem(j, R[kind][stage].shape[0])
             got, acc = R[kind][stage], ACC[kind]
             if stage == 0:
@@ -385,8 +395,7 @@
     def tile_b(j, _):
         slot = lax.rem(j, 2)
         comm(j)
-        for c in wcopies(j, slot, False):
-            c.wait()
+        pltpu.make_async_copy(wa, wa, wsem.at[slot]).wait()
         @pl.when(j + 1 < nt)
         def _():
             for c in wcopies(j + 1, 1 - slot, False):
@@ -486,8 +495,8 @@
     for n, c in [(DEPTH[0], PARTS)] + [(HOLD, PARTS >> k) for k in range(LAST)] + [(DEPTH[k], PARTS >> k) for k in range(1, LAST + 1)]:
         scratch += [V((n, c) + bu, F32), V((n, c) + bd, F32)]
     scratch += [V((PAIR,) + bu, F32), V((PAIR,) + bd, F32), V(bu, F32), V(bd, F32)]
-    flags = 2 * len(SEEN) * max(DEPTH)
-    scratch += [D((PAIR,)), D((PAIR, PAIR)), D((PAIR,)), D((flags,)), D((flags,)), D((PAIR, PAIR))]
+    flags = len(SEEN) * max(DEPTH)
+    scratch += [D((PAIR,)), D((PAIR,)), D((PAIR,)), D((flags,)), D((flags,)), D((PAIR, PAIR))]
     return pl.pallas_call(
         functools.partial(kernel_bc, (nt, nr, nc, t, ft, d, nd)),
         out_shape=(S((2 * nt,) + bu, F32), S((2 * nt,) + bd, F32), S((8, 128), F32)),

time: 617 us -> 616 us (level)
  no operation moved by 1% of the time
where the time goes in v3:
time: 616 us; the launch traced here: 615 us
  Pallas kernels  613 us (100%)
    pallas_call x1, Pallas kernels, backward(): pl.pallas_call(functools.partial(kernel_bc, (nt, nr, nc, t, ft, d, nd)),...  372 us
    pallas_call x1, Pallas kernels, update(): pl.pallas_call(functools.partial(kernel_update, (nd, pieces, ru, f // pie...  121 us
    pallas_call x1, Pallas kernels, forward_one(): pl.pallas_call(functools.partial(kernel_a, (nt, nr, rb, tr, tb, ft, d, nd...  98.2 us
    pallas_call x1, Pallas kernels, emit(): pl.pallas_call(functools.partial(kernel_emit, (nd, nt)), out_shape=[S(a.s...  21.7 us

profile of v3, /device:TPU:0, one launch (start us, length us, event | category | flops | bytes accessed | tf_op | source)
XLA Modules:
  0.0 615.0 jit_solution(1959825305944165851)
XLA Ops:
  0.7 98.2 %forward_one.1 = (f32[19,256,4096]{2,1,0:T(8,128)}, bf16[896,4096]{1,0:T(8,128)(2,1)}, bf16[896,4096]{1,0:T(8,128)(2,1)}, bf16[896,4096]{1,0:T(8,128)(2,1)}, bf16[4864,896]{1,0:T(8,128)(2,1)}) custom-call(bf16[4096,896]{1,0:T(8,128)(2,1)} %x_hbm.1, bf16[4096,896]{1,0:T(8,128)(2,1)} %e_hbm.1, bf16[896,4864]{1,0:T(8,128)(2,1)} %w1_hbm.1, ...), custom_call_target="tpu_custom_call" | custom-call | tf_op jit(solution)/shard_map/forward_one/pallas_call | solution.py:200
  98.9 371.9 %backward.1 = (f32[38,56,256]{2,1,0:T(8,128)}, f32[38,16,896]{2,1,0:T(8,128)}, f32[8,128]{1,0:T(8,128)}) custom-call(bf16[896,4096]{1,0:T(8,128)(2,1)} %get-tuple-element.47.ut_hbm, bf16[896,4096]{1,0:T(8,128)(2,1)} %get-tuple-element.48.et_hbm, bf16[896,4096]{1,0:T(8,128)(2,1)} %get-tuple-element.49.xt_hbm, f32[19,256,4096]{2,1,0:T(8,128)} %get-tuple-element.50.z_hbm, ...), custom_call_target="tpu_custom_call" | custom-call | tf_op jit(solution)/shard_map/backward/pallas_call | solution.py:500
  472.1 121.1 %update.1 = (bf16[896,4864]{1,0:T(8,128)(2,1)S(1)}, bf16[896,4864]{1,0:T(8,128)(2,1)S(1)}, bf16[4864,896]{1,0:T(8,128)(2,1)S(1)}, bf16[4864,896]{1,0:T(8,128)(2,1)S(1)}, f32[8,128]{1,0:T(8,128)S(1)}) custom-call(f32[8,128]{1,0:T(8,128)} %get-tuple-element.52.part_hbm, f32[1]{0:T(128)} %bitcast.6.rate_ref, f32[1]{0:T(128)} %bitcast.8.clip_ref, ...), custom_call_target="tpu_custom_call" | custom-call | tf_op jit(solution)/shard_map/update/pallas_call | solution.py:685
  593.2 21.7 %emit.1 = (bf16[896,4864]{1,0:T(8,128)(2,1)}, bf16[4864,896]{1,0:T(8,128)(2,1)}, bf16[896,4864]{1,0:T(8,128)(2,1)}, bf16[4864,896]{1,0:T(8,128)(2,1)}, f32[56,48...) custom-call(f32[8,128]{1,0:T(8,128)S(1)} %get-tuple-element.55.norm_, ...), custom_call_target="tpu_custom_call" | custom-call | tf_op jit(solution)/shard_map/emit/pallas_call | solution.py:746

commit v4 on v3

--- a/solution.py
+++ b/solution.py
@@ -515,7 +515,7 @@
 CORR_ONE = 1.0 - BETA_ONE ** STEP
 CORR_TWO = 1.0 - BETA_TWO ** STEP
 WIDTH = 16
-LAG = 3
+LAG = 4
 AHEAD = 2
 EMIT = 4
 UPDATE_VMEM = 19 * 1024 * 1024 + 256 * 1024

time: 616 us -> 616 us (level)
  no operation moved by 1% of the time
where the time goes in v4:
time: 616 us; the launch traced here: 615 us
  Pallas kernels  613 us (100%)
    pallas_call x1, Pallas kernels, backward(): pl.pallas_call(functools.partial(kernel_bc, (nt, nr, nc, t, ft, d, nd)),...  372 us
    pallas_call x1, Pallas kernels, update(): pl.pallas_call(functools.partial(kernel_update, (nd, pieces, ru, f // pie...  121 us
    pallas_call x1, Pallas kernels, forward_one(): pl.pallas_call(functools.partial(kernel_a, (nt, nr, rb, tr, tb, ft, d, nd...  98.2 us
    pallas_call x1, Pallas kernels, emit(): pl.pallas_call(functools.partial(kernel_emit, (nd, nt)), out_shape=[S(a.s...  21.7 us

profile of v4, /device:TPU:0, one launch (start us, length us, event | category | flops | bytes accessed | tf_op | source)
XLA Modules:
  0.0 615.0 jit_solution(13531255347623888376)
XLA Ops:
  0.7 98.2 %forward_one.1 = (f32[19,256,4096]{2,1,0:T(8,128)}, bf16[896,4096]{1,0:T(8,128)(2,1)}, bf16[896,4096]{1,0:T(8,128)(2,1)}, bf16[896,4096]{1,0:T(8,128)(2,1)}, bf16[4864,896]{1,0:T(8,128)(2,1)}) custom-call(bf16[4096,896]{1,0:T(8,128)(2,1)} %x_hbm.1, bf16[4096,896]{1,0:T(8,128)(2,1)} %e_hbm.1, bf16[896,4864]{1,0:T(8,128)(2,1)} %w1_hbm.1, ...), custom_call_target="tpu_custom_call" | custom-call | tf_op jit(solution)/shard_map/forward_one/pallas_call | solution.py:200
  98.9 371.9 %backward.1 = (f32[38,56,256]{2,1,0:T(8,128)}, f32[38,16,896]{2,1,0:T(8,128)}, f32[8,128]{1,0:T(8,128)}) custom-call(bf16[896,4096]{1,0:T(8,128)(2,1)} %get-tuple-element.47.ut_hbm, bf16[896,4096]{1,0:T(8,128)(2,1)} %get-tuple-element.48.et_hbm, bf16[896,4096]{1,0:T(8,128)(2,1)} %get-tuple-element.49.xt_hbm, f32[19,256,4096]{2,1,0:T(8,128)} %get-tuple-element.50.z_hbm, ...), custom_call_target="tpu_custom_call" | custom-call | tf_op jit(solution)/shard_map/backward/pallas_call | solution.py:500
  472.1 121.0 %update.1 = (bf16[896,4864]{1,0:T(8,128)(2,1)S(1)}, bf16[896,4864]{1,0:T(8,128)(2,1)S(1)}, bf16[4864,896]{1,0:T(8,128)(2,1)S(1)}, bf16[4864,896]{1,0:T(8,128)(2,1)S(1)}, f32[8,128]{1,0:T(8,128)S(1)}) custom-call(f32[8,128]{1,0:T(8,128)} %get-tuple-element.52.part_hbm, f32[1]{0:T(128)} %bitcast.6.rate_ref, f32[1]{0:T(128)} %bitcast.8.clip_ref, ...), custom_call_target="tpu_custom_call" | custom-call | tf_op jit(solution)/shard_map/update/pallas_call | solution.py:685
  593.1 21.7 %emit.1 = (bf16[896,4864]{1,0:T(8,128)(2,1)}, bf16[4864,896]{1,0:T(8,128)(2,1)}, bf16[896,4864]{1,0:T(8,128)(2,1)}, bf16[4864,896]{1,0:T(8,128)(2,1)}, f32[56,48...) custom-call(f32[8,128]{1,0:T(8,128)S(1)} %get-tuple-element.55.norm_, ...), custom_call_target="tpu_custom_call" | custom-call | tf_op jit(solution)/shard_map/emit/pallas_call | solution.py:746
